TPU v7x, 32 devices: a whole 2x2x4 slice. The times are simulated.
32 devices in a mesh: grp: 2 (over core), tp: 4 (over y, x), src: 4 (over z).
Axes of the slice: x: 2, y: 2, z: 4, core: 2. Of those that a mesh axis runs over, the one named last changes fastest.
Arguments:
- hidden_in: bfloat16 [512, 5120], P(('grp', 'src')), may hold values from -6 to 6
- attn_gain: float32 [5120], replicated, may hold values from 0.5 to 1.5
- w_qkv: int32 [1280, 5120], P(None, 'tp'), may hold values from -2147483648 to 2147483646
- qkv_scale: float32 [5120], P('tp'), may hold values from 0.0001118034 to 0.00041926274
- q_gain: float32 [128], replicated, may hold values from 0.25 to 1.75
- k_gain: float32 [128], replicated, may hold values from 0.1 to 1.9
- key_cache: bfloat16 [8, 64, 128, 512], P(('grp', 'src'), 'tp'), may hold values from -400 to 400
- value_cache: bfloat16 [8, 64, 128, 512], P(('grp', 'src'), 'tp'), may hold values from -9 to 9
- lengths: int32 [8, 64], P(('grp', 'src'), 'tp'), may hold values from 1 to 128, as said below
- w_out: int32 [1024, 5120], P('tp'), may hold values from -2147483648 to 2147483646
- out_scale: float32 [5120], replicated, may hold values from 0.0003125 to 0.00125
- mlp_gain: float32 [5120], replicated, may hold values from 0.5 to 1.5
- w_gate: int32 [1280, 12800], P(('grp', 'src'), 'tp'), may hold values from -2147483648 to 2147483646
- w_up: int32 [1280, 12800], P(('grp', 'src'), 'tp'), may hold values from -2147483648 to 2147483646
- gate_scale: float32 [12800], P('tp'), may hold values from 0.0001118034 to 0.00041926274
- up_scale: float32 [12800], P('tp'), may hold values from 0.0001118034 to 0.00041926274
- w_down: int32 [3200, 5120], P('tp', ('grp', 'src')), may hold values from -2147483648 to 2147483646
- down_scale: float32 [5120], replicated, may hold values from 0.00013258251 to 0.00053033006
Outputs:
- layer_out: bfloat16 [512, 5120], P(('grp', 'src'), 'tp')
Inputs may be any that keep to these rules, and one draw needn't show every extreme that they name: `lengths`: some sequence has exactly 128 cached positions.
All inputs are finite; a program needn't handle non-finite values.
Results may differ from a plain program's by a relative error of at most 0.028.
Values may be sent and summed in bfloat16 or wider, within the bound.
A program may use at most 128 MiB of HBM per device.

v0:
```python
import math
import jax
import jax.numpy as jnp
from jax import lax
from jax.sharding import PartitionSpec as P

D = 5120
QUERY_HEADS = 32
KEY_VALUE_HEADS = 4
HEAD_SIZE = 128
QUERY_COLUMNS = 4096
KEY_COLUMNS = 512
norm_epsilon = 1e-06
rope_base = 1000000.0


def unpack_bytes(packed, byte_index):
    return jnp.right_shift(jnp.left_shift(packed, 24 - 8 * byte_index), 24)


def byte_product(activations, packed):
    products = [
        jnp.dot(
            activations[:, byte_index::4],
            unpack_bytes(packed, byte_index).astype(jnp.bfloat16),
            preferred_element_type=jnp.float32,
        )
        for byte_index in range(4)
    ]
    return products[0] + products[1] + products[2] + products[3]


def normalize_rows(values, gain_row):
    return (
        values
        * lax.rsqrt(jnp.mean(values * values, axis=-1, keepdims=True) + norm_epsilon)
        * gain_row
    )


def rotary_embed(values, positions):
    half_dim = values.shape[-1] // 2
    freq_index = jnp.arange(half_dim, dtype=jnp.float32)
    inverse = jnp.exp(freq_index * (-math.log(rope_base) / half_dim))
    angles = positions.astype(jnp.float32)[:, None] * inverse[None, :]
    cosine = jnp.cos(angles)[:, None, :]
    sine_part = jnp.sin(angles)[:, None, :]
    lower_half = values[..., :half_dim]
    upper_half = values[..., half_dim:]
    return jnp.concatenate(
        [
            lower_half * cosine - upper_half * sine_part,
            upper_half * cosine + lower_half * sine_part,
        ],
        axis=-1,
    )


def local_attention(query_key_value_rows, q_gain, k_gain, stored_keys, stored_values, seq_lengths):
    count_of_rows = query_key_value_rows.shape[0]
    cache_length = stored_keys.shape[1]
    query_matrix = (
        query_key_value_rows[:, :QUERY_COLUMNS]
        .astype(jnp.float32)
        .reshape(count_of_rows, QUERY_HEADS, HEAD_SIZE)
    )
    incoming_keys = (
        query_key_value_rows[:, QUERY_COLUMNS : QUERY_COLUMNS + KEY_COLUMNS]
        .astype(jnp.float32)
        .reshape(count_of_rows, KEY_VALUE_HEADS, HEAD_SIZE)
    )
    incoming_values = query_key_value_rows[:, QUERY_COLUMNS + KEY_COLUMNS :].reshape(
        count_of_rows, KEY_VALUE_HEADS, HEAD_SIZE
    )
    query_matrix = rotary_embed(normalize_rows(query_matrix, q_gain), seq_lengths).astype(
        jnp.bfloat16
    )
    incoming_keys = rotary_embed(normalize_rows(incoming_keys, k_gain), seq_lengths).astype(
        jnp.bfloat16
    )
    query_groups = query_matrix.reshape(
        count_of_rows, KEY_VALUE_HEADS, QUERY_HEADS // KEY_VALUE_HEADS, HEAD_SIZE
    )
    key_slices = stored_keys.reshape(count_of_rows, cache_length, KEY_VALUE_HEADS, HEAD_SIZE)
    value_slices = stored_values.reshape(count_of_rows, cache_length, KEY_VALUE_HEADS, HEAD_SIZE)
    logit_scale = 1.0 / math.sqrt(HEAD_SIZE)
    scores = (
        jnp.einsum("bkgd,bpkd->bkgp", query_groups, key_slices, preferred_element_type=jnp.float32)
        * logit_scale
    )
    live_mask = jnp.arange(cache_length, dtype=jnp.int32)[None, :] < seq_lengths[:, None]
    scores = jnp.where(live_mask[:, None, None, :], scores, -jnp.inf)
    self_score = (
        jnp.einsum("nufi,nui->nuf", query_groups, incoming_keys, preferred_element_type=jnp.float32)
        * logit_scale
    )
    row_max = jnp.maximum(jnp.max(scores, axis=-1), self_score)
    soft_weights = jnp.exp(scores - row_max[..., None])
    own_weight = jnp.exp(self_score - row_max)
    denominator = jnp.sum(soft_weights, axis=-1) + own_weight
    own_low = lax.optimization_barrier(own_weight.astype(jnp.bfloat16)).astype(jnp.float32)
    numerator = jnp.einsum(
        "bkgp,bpkd->bkgd",
        soft_weights.astype(jnp.bfloat16),
        value_slices,
        preferred_element_type=jnp.float32,
    )
    numerator = numerator + own_low[..., None] * incoming_values.astype(jnp.float32)[:, :, None, :]
    return (
        (numerator / denominator[..., None])
        .reshape(count_of_rows, QUERY_COLUMNS)
        .astype(jnp.bfloat16)
    )


def local(
    hidden_in,
    attn_gain,
    w_qkv,
    qkv_scale,
    q_gain,
    k_gain,
    key_cache,
    value_cache,
    lengths,
    w_out,
    out_scale,
    mlp_gain,
    w_gate,
    w_up,
    gate_scale,
    up_scale,
    w_down,
    down_scale,
):
    tp_count = lax.axis_size("tp")
    tp_index = lax.axis_index("tp")
    share_cols = D // tp_count
    residual = hidden_in.astype(jnp.float32)
    normed = normalize_rows(residual, attn_gain).astype(jnp.bfloat16)
    qkv_part = (byte_product(normed, w_qkv) * qkv_scale).astype(jnp.bfloat16)
    query_key_value_rows = lax.all_to_all(qkv_part, "tp", split_axis=0, concat_axis=1, tiled=True)
    heads_out = local_attention(
        query_key_value_rows, q_gain, k_gain, key_cache[0], value_cache[0], lengths[0]
    )
    head_rows = lax.all_to_all(heads_out, "tp", split_axis=1, concat_axis=0, tiled=True)
    partial_value = byte_product(head_rows, w_out) * out_scale
    attn_full = lax.psum(partial_value.astype(jnp.bfloat16), "tp").astype(jnp.float32)
    mid_full = (residual + attn_full).astype(jnp.bfloat16)
    normed_mlp = normalize_rows(mid_full.astype(jnp.float32), mlp_gain).astype(jnp.bfloat16)
    mid_share = lax.dynamic_slice_in_dim(mid_full, tp_index * share_cols, share_cols, 1)
    gate_total = byte_product(
        normed_mlp, lax.all_gather(w_gate, ("grp", "src"), axis=0, tiled=True)
    )
    up_total = byte_product(normed_mlp, lax.all_gather(w_up, ("grp", "src"), axis=0, tiled=True))
    activated = (jax.nn.silu(gate_total * gate_scale) * (up_total * up_scale)).astype(jnp.bfloat16)
    down_terms = (
        byte_product(activated, lax.all_gather(w_down, ("grp", "src"), axis=1, tiled=True))
        * down_scale
    )
    mlp_share = lax.psum_scatter(
        down_terms.astype(jnp.bfloat16), "tp", scatter_dimension=1, tiled=True
    ).astype(jnp.float32)
    return (mid_share.astype(jnp.float32) + mlp_share).astype(jnp.bfloat16)


def solution(mesh):
    return jax.shard_map(
        local,
        mesh=mesh,
        in_specs=(
            P(("grp", "src"), None),
            P(),
            P(None, "tp"),
            P("tp"),
            P(),
            P(),
            P(("grp", "src"), "tp", None, None),
            P(("grp", "src"), "tp", None, None),
            P(("grp", "src"), "tp"),
            P("tp", None),
            P(),
            P(),
            P(("grp", "src"), "tp"),
            P(("grp", "src"), "tp"),
            P("tp"),
            P("tp"),
            P("tp", ("grp", "src")),
            P(),
        ),
        out_specs=P(("grp", "src"), "tp"),
        check_vma=False,
    )
```

profile of v0, /device:TPU:0, one launch (start us, length us, event | category | flops | bytes accessed | tf_op | source)
XLA Modules:
  0.0 582.0 jit_solution(6829318386932394782)
XLA Ops:
  7.4 1.3 fusion.81
  8.7 1.3 fusion.83
  10.0 6.5 %slice.73 = bf16[64,1280]{1,0:T(8,128)(2,1)S(1)} slice(bf16[64,5120]{1,0:T(8,128)(2,1)S(1)} %fusion.83), slice={[0:64:1], [0:5120:4]} | slice | bytes 327680 | tf_op jit(solution)/shard_map/slice | solution.py:24
  16.6 6.6 %slice.74 = bf16[64,1280]{1,0:T(8,128)(2,1)S(1)} slice(bf16[64,5120]{1,0:T(8,128)(2,1)S(1)} %fusion.83), slice={[0:64:1], [1:5120:4]} | slice | bytes 327680 | tf_op jit(solution)/shard_map/slice | solution.py:24
  23.1 6.5 %slice.75 = bf16[64,1280]{1,0:T(8,128)(2,1)S(1)} slice(bf16[64,5120]{1,0:T(8,128)(2,1)S(1)} %fusion.83), slice={[0:64:1], [2:5120:4]} | slice | bytes 327680 | tf_op jit(solution)/shard_map/slice | solution.py:24
  29.6 6.7 %slice.76 = bf16[64,1280]{1,0:T(8,128)(2,1)S(1)} slice(bf16[64,5120]{1,0:T(8,128)(2,1)S(1)} %fusion.83), slice={[0:64:1], [3:5120:4]} | slice | bytes 327680 | tf_op jit(solution)/shard_map/slice | solution.py:24
  36.4 4.0 fusion.50
  43.2 1.5 fusion.73
  44.8 5.3 all-to-all-start
  50.1 2.6 reshape_squeeze.6
  52.7 4.0 reshape_squeeze.7
  58.1 1.3 fusion.148
  59.9 2.3 fusion.97
  62.3 9.2 %all_to_all.35 = bf16[16,4,1024]{2,0,1:T(8,128)(2,1)S(1)} all-to-all(bf16[16,4,1024]{2,0,1:T(8,128)(2,1)S(1)} %copy.28), channel_id=1, replica_groups=mesh['grp'=2,'tp'=4,'src'=4] {'tp'}, dimensions={1} | all-to-all | bytes 262144 | tf_op jit(solution)/shard_map/all_to_all | solution.py:146
  71.5 1.1 slice.84
  72.7 1.1 slice.85
  73.8 1.1 slice.86
  76.1 3.5 fusion.61
  79.6 3.5 convolution_add_fusion.2
  84.0 1.6 fusion.39
  87.5 44.9 %all-reduce.2.cloned.1.call-done = bf16[64,5120]{1,0:T(8,128)(2,1)} async-done(((bf16[64,5120]{1,0:T(8,128)(2,1)}), bf16[64,5120]{1,0:T(8,128)(2,1)}) %all-reduce.2.cloned.1.call-update) | async-done | bytes 655376 | tf_op jit(solution)/shard_map/psum | solution.py:148
  132.4 1.4 fusion.78
  134.0 7.0 %slice.88 = bf16[64,1280]{1,0:T(8,128)(2,1)S(1)} slice(bf16[64,5120]{1,0:T(8,128)(2,1)S(1)} %fusion.80), slice={[0:64:1], [0:5120:4]} | slice | bytes 327680 | tf_op jit(solution)/shard_map/slice | solution.py:24
  141.0 6.6 %slice.89 = bf16[64,1280]{1,0:T(8,128)(2,1)S(1)} slice(bf16[64,5120]{1,0:T(8,128)(2,1)S(1)} %fusion.80), slice={[0:64:1], [1:5120:4]} | slice | bytes 327680 | tf_op jit(solution)/shard_map/slice | solution.py:24
  147.6 6.5 %slice.90 = bf16[64,1280]{1,0:T(8,128)(2,1)S(1)} slice(bf16[64,5120]{1,0:T(8,128)(2,1)S(1)} %fusion.80), slice={[0:64:1], [2:5120:4]} | slice | bytes 327680 | tf_op jit(solution)/shard_map/slice | solution.py:24
  154.1 6.7 %slice.91 = bf16[64,1280]{1,0:T(8,128)(2,1)S(1)} slice(bf16[64,5120]{1,0:T(8,128)(2,1)S(1)} %fusion.80), slice={[0:64:1], [3:5120:4]} | slice | bytes 327680 | tf_op jit(solution)/shard_map/slice | solution.py:24
  160.8 74.5 %all-gather.4.cloned.1.call-done = s32[1280,3200]{1,0:T(8,128)} async-done(((s32[160,3200]{1,0:T(8,128)}), s32[1280,3200]{1,0:T(8,128)}) %all-gather.4.cloned.1.call-update) | async-done | bytes 16384016 | tf_op jit(solution)/shard_map/all_gather | solution.py:153
  235.3 8.0 %fusion = f32[64,3200]{1,0:T(8,128)S(1)} fusion(bf16[64,1280]{1,0:T(8,128)(2,1)S(1)} %slice.88, s32[1280,3200]{1,0:T(8,128)} %all-gather.4.cloned.1.call-done), kind=kOutput, calls=%fused_computation.12 | convolution fusion | flops 536576000 | bytes 17367040 | tf_op jit(solution)/shard_map/dot_general | solution.py:23
  243.3 139.4 %all-gather.6.cloned.1.call-done = s32[1280,3200]{1,0:T(8,128)} async-done(((s32[160,3200]{1,0:T(8,128)}), s32[1280,3200]{1,0:T(8,128)}) %all-gather.6.cloned.1.call-update) | async-done | bytes 16384016 | tf_op jit(solution)/shard_map/all_gather | solution.py:155
  382.7 8.1 %fusion.4 = f32[64,3200]{1,0:T(8,128)S(1)} fusion(bf16[64,1280]{1,0:T(8,128)(2,1)S(1)} %slice.88, s32[1280,3200]{1,0:T(8,128)} %all-gather.6.cloned.1.call-done), kind=kOutput, calls=%fused_computation.16 | convolution fusion | flops 536576000 | bytes 17367040 | tf_op jit(solution)/shard_map/dot_general | solution.py:23
  390.8 9.9 %fusion.45 = f32[64,3200]{1,0:T(8,128)S(1)} fusion(f32[64,3200]{1,0:T(8,128)S(1)} %fusion, bf16[64,1280]{1,0:T(8,128)(2,1)S(1)} %slice.89, s32[1280,3200]{1,0:T(8,128)} %all-gather.4.cloned.1.call-done), kind=kOutput, calls=%fused_computation.68 | convolution fusion | flops 536780800 | bytes 18186240 | tf_op jit(solution)/shard_map/dot_general | solution.py:23
  400.8 2.4 fusion.42
  403.2 8.0 %fusion.44 = f32[64,3200]{1,0:T(8,128)S(1)} fusion(f32[64,3200]{1,0:T(8,128)S(1)} %fusion.45, bf16[64,1280]{1,0:T(8,128)(2,1)S(1)} %slice.90, s32[1280,3200]{1,0:T(8,128)} %all-gather.4.cloned.1.call-done), kind=kOutput, calls=%fused_computation.67 | convolution fusion | flops 536780800 | bytes 18186240 | tf_op jit(solution)/shard_map/dot_general | solution.py:23
  411.2 2.6 fusion.41
  413.9 7.6 %fusion.46 = f32[64,3200]{1,0:T(8,128)S(1)} fusion(f32[64,3200]{1,0:T(8,128)S(1)} %fusion.44, bf16[64,1280]{1,0:T(8,128)(2,1)S(1)} %slice.91, s32[1280,3200]{1,0:T(8,128)} %all-gather.4.cloned.1.call-done, f32[3200]{0:T(1024)S(1)} %copy-done.7), kind=kOutput, calls=%fused_computation.69 | convolution fusion | flops 536985600 | bytes 18199040 | tf_op jit(solution)/shard_map/dot_general | solution.py:23
  421.5 2.0 fusion.49
  423.5 3.7 slice.92
  427.2 3.7 slice.93
  430.9 3.7 slice.94
  434.6 4.0 slice.95
  438.6 91.5 %all-gather.8.cloned.1.call-done = s32[800,5120]{1,0:T(8,128)} async-done(((s32[800,640]{1,0:T(8,128)}), s32[800,5120]{1,0:T(8,128)}) %all-gather.8.cloned.1.call-update) | async-done | bytes 16384016 | tf_op jit(solution)/shard_map/all_gather | solution.py:158
  530.1 8.2 %fusion.8 = f32[64,5120]{1,0:T(8,128)S(1)} fusion(bf16[64,800]{1,0:T(8,128)(2,1)S(1)} %slice.92, s32[800,5120]{1,0:T(8,128)} %all-gather.8.cloned.1.call-done), kind=kOutput, calls=%fused_computation.20 | convolution fusion | flops 536576000 | bytes 17797120 | tf_op jit(solution)/shard_map/dot_general | solution.py:23
  538.3 2.1 copy-done
  540.4 2.5 fusion.36
  542.9 2.5 fusion.35
  545.4 2.9 fusion.38
  548.3 24.0 %reduce-scatter.2.cloned.1.call-done = bf16[64,1280]{1,0:T(8,128)(2,1)} async-done(((bf16[64,5120]{1,0:T(8,128)(2,1)}), bf16[64,1280]{1,0:T(8,128)(2,1)}) %reduce-scatter.2.cloned.1.call-update) | async-done | bytes 163856 | tf_op jit(solution)/shard_map/reduce_scatter | solution.py:161
  572.3 1.6 add_convert_fusion
  (81 shorter events, 8.8 us)
Async XLA Ops:
  36.4 4.7 copy-start.1
  41.1 2.1 copy-start.8
  42.2 8.0 %copy-start.11 = (s32[1,16]{1,0:T(1,128)S(1)}, s32[1,16]{1,0:T(1,128)}, u32[]{:S(2)}) copy-start(s32[1,16]{1,0:T(1,128)} %param.26) | copy-start | bytes 196
  44.8 12.5 %copy-start.9 = (f32[128]{0:T(128)S(1)}, f32[128]{0:T(128)}, u32[]{:S(2)}) copy-start(f32[128]{0:T(128)} %param.23) | copy-start | bytes 1540
  44.8 12.6 %copy-start.10 = (f32[128]{0:T(128)S(1)}, f32[128]{0:T(128)}, u32[]{:S(2)}) copy-start(f32[128]{0:T(128)} %param.22) | copy-start | bytes 1540
  44.8 12.1 %all-to-all-start = ((bf16[4,16,1280]{2,1,0:T(8,128)(2,1)}), bf16[4,16,1280]{2,1,0:T(8,128)(2,1)S(1)}, u32[]{:S(2)}, u32[]{:S(2)}) async-start(bf16[4,16,1280]{2,1,0:T(8,128)(2,1)} %bitcast.1), calls=%async_computation | async-start | bytes 327680 | tf_op jit(solution)/shard_map/all_to_all | solution.py:142
  50.1 82.3 %all-reduce.2.cloned.1.call-start = ((), (), s32[]{:S(2)}) async-start(), calls=%async_computation.3 | async-start | bytes 1310720 | tf_op jit(solution)/shard_map/psum | solution.py:148
  76.1 7.0 %slice-start.4 = ((s8[5242880]{0:T(1024)(128)(4,1)}), s8[4194304]{0:T(1024)(128)(4,1)S(1)}, s32[]{:S(2)}) async-start(s8[5242880]{0:T(1024)(128)(4,1)} %bitcast.49), calls=%async_computation.12 | async-start | bytes 8388608
  79.6 3.5 slice-start.5
  79.6 4.4 copy-start.4
  84.0 48.3 %copy-start.2 = (bf16[64,5120]{1,0:T(8,128)(2,1)S(1)}, bf16[64,5120]{1,0:T(8,128)(2,1)}, u32[]{:S(2)}) copy-start(bf16[64,5120]{1,0:T(8,128)(2,1)} %param.18) | copy-start | bytes 1966084
  84.0 49.8 %copy-start.5 = (f32[5120]{0:T(1024)S(1)}, f32[5120]{0:T(1024)}, u32[]{:S(2)}) copy-start(f32[5120]{0:T(1024)} %param.29) | copy-start | bytes 61444
  85.7 149.6 %all-gather.4.cloned.1.call-start = ((), (), s32[]{:S(2)}) async-start(), calls=%async_computation.4 | async-start | bytes 18432000 | tf_op jit(solution)/shard_map/all_gather | solution.py:153
  86.3 296.4 %all-gather.6.cloned.1.call-start = ((), (), s32[]{:S(2)}) async-start(), calls=%async_computation.5 | async-start | bytes 18432000 | tf_op jit(solution)/shard_map/all_gather | solution.py:155
  86.9 443.2 %all-gather.8.cloned.1.call-start = ((), (), s32[]{:S(2)}) async-start(), calls=%async_computation.6 | async-start | bytes 18432000 | tf_op jit(solution)/shard_map/all_gather | solution.py:158
  87.4 484.9 %reduce-scatter.2.cloned.1.call-start = ((), (), s32[]{:S(2)}) async-start(), calls=%async_computation.7 | async-start | bytes 819200 | tf_op jit(solution)/shard_map/reduce_scatter | solution.py:161
  382.7 18.1 %slice-start = ((s8[16384000]{0:T(1024)(128)(4,1)}), s8[4194304]{0:T(1024)(128)(4,1)S(1)}, s32[]{:S(2)}) async-start(s8[16384000]{0:T(1024)(128)(4,1)} %bitcast.47), calls=%async_computation.8 | async-start | bytes 8388608
  382.7 18.1 %slice-start.1 = ((s8[16384000]{0:T(1024)(128)(4,1)}), s8[4194304]{0:T(1024)(128)(4,1)S(1)}, s32[]{:S(2)}) async-start(s8[16384000]{0:T(1024)(128)(4,1)} %bitcast.47), calls=%async_computation.9 | async-start | bytes 8388608
  390.8 9.9 %slice-start.2 = ((s8[16384000]{0:T(1024)(128)(4,1)}), s8[4194304]{0:T(1024)(128)(4,1)S(1)}, s32[]{:S(2)}) async-start(s8[16384000]{0:T(1024)(128)(4,1)} %bitcast.47), calls=%async_computation.10 | async-start | bytes 8388608
  390.8 9.9 %slice-start.3 = ((s8[16384000]{0:T(1024)(128)(4,1)}), s8[3801088]{0:T(1024)(128)(4,1)S(1)}, s32[]{:S(2)}) async-start(s8[16384000]{0:T(1024)(128)(4,1)} %bitcast.47), calls=%async_computation.11 | async-start | bytes 7602176
  411.2 2.6 copy-start.7
  413.9 7.6 %copy-start.6 = (f32[3200]{0:T(1024)S(1)}, f32[3200]{0:T(1024)}, u32[]{:S(2)}) copy-start(f32[3200]{0:T(1024)} %param.33) | copy-start | bytes 38404
  530.1 10.3 %copy-start = (s32[800,5120]{1,0:T(8,128)S(1)}, s32[800,5120]{1,0:T(8,128)}, u32[]{:S(2)}) copy-start(s32[800,5120]{1,0:T(8,128)} %all-gather.8.cloned.1.call-done) | copy-start | bytes 49152004
  542.9 2.5 copy-start.3
Sparse Core Ops, SparseCore 0:
  85.8 46.4 all-reduce.1
  548.4 23.8 reduce-scatter.1
Sparse Core Ops, SparseCore 1:
  87.8 147.4 all-gather.3
  236.7 145.9 all-gather.5
  384.2 145.9 all-gather.7
where the time goes:
time: 589 us; the launch traced here: 582 us
  waiting for transfers between devices  376 us (64%)
  matrix products  85.7 us (15%)
  local copies, waits for them, and re-layouts  82.3 us (14%)
  between operations  16.1 us (3%)
  blocking collectives  9.25 us (2%)
  other arithmetic  7.26 us (1%)
    all_gather x1, waiting for transfers between devices, local(): lax.all_gather(w_up, ('grp', 'src'), axis=0, tiled=True)  139 us
    all_gather x1, waiting for transfers between devices, local(): lax.all_gather(w_down, ('grp', 'src'), axis=1, tiled=True)  91.5 us
    dot_general x20, matrix products, byte_product(): jnp.dot(activations[:, byte_index::4], unpack_bytes(packed, byte_index).a...  81.8 us
    all_gather x1, waiting for transfers between devices, local(): lax.all_gather(w_gate, ('grp', 'src'), axis=0, tiled=True)  74.5 us
    slice x16, local copies, waits for them, and re-layouts, byte_product(): activations[:, byte_index::4]  72.7 us
    psum x1, waiting for transfers between devices, local(): lax.psum(partial_value.astype(jnp.bfloat16), 'tp').astype(jnp.float32)  44.9 us
    reduce_scatter x1, waiting for transfers between devices, local(): lax.psum_scatter(down_terms.astype(jnp.bfloat16), 'tp', scatter_dimension...  24 us
  transfers between devices with their start and end apart: 6, of which 5 were waited for; matrix products, arithmetic and copies ran while one was open for 17% of the time, Pallas kernels for 0%

commit v1 on v0

--- a/solution.py
+++ b/solution.py
@@ -12,6 +12,7 @@
 KEY_COLUMNS = 512
 norm_epsilon = 1e-06
 rope_base = 1000000.0
+tiles_hold = lambda load, axis_id: lax.all_gather(load, axis_id).sum(axis=0)
 
 
 def unpack_bytes(packed, byte_index):
@@ -145,7 +146,7 @@
     )
     head_rows = lax.all_to_all(heads_out, "tp", split_axis=1, concat_axis=0, tiled=True)
     partial_value = byte_product(head_rows, w_out) * out_scale
-    attn_full = lax.psum(partial_value.astype(jnp.bfloat16), "tp").astype(jnp.float32)
+    attn_full = tiles_hold(partial_value.astype(jnp.bfloat16), "tp").astype(jnp.float32)
     mid_full = (residual + attn_full).astype(jnp.bfloat16)
     normed_mlp = normalize_rows(mid_full.astype(jnp.float32), mlp_gain).astype(jnp.bfloat16)
     mid_share = lax.dynamic_slice_in_dim(mid_full, tp_index * share_cols, share_cols, 1)

time: 589 us -> 629 us (1.068)
  waiting for transfers between devices: 376 us -> 414 us
    all_gather x1, waiting for transfers between devices: 74.5 us -> 120 us  [local(): lax.all_gather(w_gate, ('grp', 'src'), axis=0, tiled=True)]
    psum x1 -> x0, waiting for transfers between devices: 44.9 us -> none  [local(): lax.psum(partial_value.astype(jnp.bfloat16), 'tp').astype(jnp.float32)]
    all_gather x0 -> x1, waiting for transfers between devices: none -> 37.3 us  [tiles_hold = lambda load, axis_id: lax.all_gather(load, axis_id).sum(axis=0)]
  transfers between devices with their start and end apart: 6 -> 6, of which waited for: 5 -> 5; matrix products, arithmetic and copies ran while one was open for 17% -> 16% of each run, Pallas kernels for 0% -> 0%
where the time goes in v1:
time: 629 us; the launch traced here: 620 us
  waiting for transfers between devices  414 us (66%)
  matrix products  85.7 us (14%)
  local copies, waits for them, and re-layouts  82.3 us (13%)
  between operations  14.2 us (2%)
  blocking collectives  9.01 us (1%)
  other arithmetic  8.41 us (1%)
    all_gather x1, waiting for transfers between devices, local(): lax.all_gather(w_up, ('grp', 'src'), axis=0, tiled=True)  140 us
    all_gather x1, waiting for transfers between devices, local(): lax.all_gather(w_gate, ('grp', 'src'), axis=0, tiled=True)  120 us
    all_gather x1, waiting for transfers between devices, local(): lax.all_gather(w_down, ('grp', 'src'), axis=1, tiled=True)  91.6 us
    dot_general x20, matrix products, byte_product(): jnp.dot(activations[:, byte_index::4], unpack_bytes(packed, byte_index).a...  81.8 us
    slice x16, local copies, waits for them, and re-layouts, byte_product(): activations[:, byte_index::4]  72.4 us
    all_gather x1, waiting for transfers between devices, tiles_hold = lambda load, axis_id: lax.all_gather(load, axis_id).sum(axis=0)  37.3 us
    reduce_scatter x1, waiting for transfers between devices, local(): lax.psum_scatter(down_terms.astype(jnp.bfloat16), 'tp', scatter_dimension...  24 us
  transfers between devices with their start and end apart: 6, of which 5 were waited for; matrix products, arithmetic and copies ran while one was open for 16% of the time, Pallas kernels for 0%

profile of v1, /device:TPU:0, one launch (start us, length us, event | category | flops | bytes accessed | tf_op | source)
XLA Modules:
  0.0 619.5 jit_solution(17203893072316480046)
XLA Ops:
  6.5 1.3 fusion.81
  7.9 1.3 fusion.83
  9.2 6.5 %slice.73 = bf16[64,1280]{1,0:T(8,128)(2,1)S(1)} slice(bf16[64,5120]{1,0:T(8,128)(2,1)S(1)} %fusion.83), slice={[0:64:1], [0:5120:4]} | slice | bytes 327680 | tf_op jit(solution)/shard_map/slice | solution.py:25
  15.7 6.6 %slice.74 = bf16[64,1280]{1,0:T(8,128)(2,1)S(1)} slice(bf16[64,5120]{1,0:T(8,128)(2,1)S(1)} %fusion.83), slice={[0:64:1], [1:5120:4]} | slice | bytes 327680 | tf_op jit(solution)/shard_map/slice | solution.py:25
  22.3 6.5 %slice.75 = bf16[64,1280]{1,0:T(8,128)(2,1)S(1)} slice(bf16[64,5120]{1,0:T(8,128)(2,1)S(1)} %fusion.83), slice={[0:64:1], [2:5120:4]} | slice | bytes 327680 | tf_op jit(solution)/shard_map/slice | solution.py:25
  28.8 6.5 %slice.76 = bf16[64,1280]{1,0:T(8,128)(2,1)S(1)} slice(bf16[64,5120]{1,0:T(8,128)(2,1)S(1)} %fusion.83), slice={[0:64:1], [3:5120:4]} | slice | bytes 327680 | tf_op jit(solution)/shard_map/slice | solution.py:25
  35.3 4.0 fusion.50
  42.2 1.5 fusion.73
  43.7 5.3 all-to-all-start
  49.1 2.8 reshape_squeeze.6
  51.9 4.0 reshape_squeeze.7
  57.3 1.3 fusion.148
  59.0 2.3 fusion.97
  61.4 9.0 %all_to_all.35 = bf16[16,4,1024]{2,0,1:T(8,128)(2,1)S(1)} all-to-all(bf16[16,4,1024]{2,0,1:T(8,128)(2,1)S(1)} %copy.28), channel_id=1, replica_groups=mesh['grp'=2,'tp'=4,'src'=4] {'tp'}, dimensions={1} | all-to-all | bytes 262144 | tf_op jit(solution)/shard_map/all_to_all | solution.py:147
  70.5 1.1 slice.84
  71.6 1.1 slice.85
  72.8 1.1 slice.86
  75.1 3.5 fusion.61
  78.6 3.5 convolution_add_fusion.2
  83.0 1.6 fusion.39
  86.7 37.3 %all-gather.12.cloned.1.call-done = bf16[256,5120]{1,0:T(8,128)(2,1)} async-done(((bf16[64,5120]{1,0:T(8,128)(2,1)}), bf16[256,5120]{1,0:T(8,128)(2,1)}) %all-gather.12.cloned.1.call-update) | async-done | bytes 2621456 | tf_op jit(solution)/shard_map/all_gather | solution.py:15
  124.0 2.2 reduce_sum.61
  126.8 6.9 %slice.88 = bf16[64,1280]{1,0:T(8,128)(2,1)S(1)} slice(bf16[64,5120]{1,0:T(8,128)(2,1)S(1)} %fusion.80), slice={[0:64:1], [0:5120:4]} | slice | bytes 327680 | tf_op jit(solution)/shard_map/slice | solution.py:25
  133.8 6.6 %slice.89 = bf16[64,1280]{1,0:T(8,128)(2,1)S(1)} slice(bf16[64,5120]{1,0:T(8,128)(2,1)S(1)} %fusion.80), slice={[0:64:1], [1:5120:4]} | slice | bytes 327680 | tf_op jit(solution)/shard_map/slice | solution.py:25
  140.3 6.5 %slice.90 = bf16[64,1280]{1,0:T(8,128)(2,1)S(1)} slice(bf16[64,5120]{1,0:T(8,128)(2,1)S(1)} %fusion.80), slice={[0:64:1], [2:5120:4]} | slice | bytes 327680 | tf_op jit(solution)/shard_map/slice | solution.py:25
  146.8 6.7 %slice.91 = bf16[64,1280]{1,0:T(8,128)(2,1)S(1)} slice(bf16[64,5120]{1,0:T(8,128)(2,1)S(1)} %fusion.80), slice={[0:64:1], [3:5120:4]} | slice | bytes 327680 | tf_op jit(solution)/shard_map/slice | solution.py:25
  153.5 119.9 %all-gather.6.cloned.1.call-done = s32[1280,3200]{1,0:T(8,128)} async-done(((s32[160,3200]{1,0:T(8,128)}), s32[1280,3200]{1,0:T(8,128)}) %all-gather.6.cloned.1.call-update) | async-done | bytes 16384016 | tf_op jit(solution)/shard_map/all_gather | solution.py:154
  273.5 8.0 %fusion = f32[64,3200]{1,0:T(8,128)S(1)} fusion(bf16[64,1280]{1,0:T(8,128)(2,1)S(1)} %slice.88, s32[1280,3200]{1,0:T(8,128)} %all-gather.6.cloned.1.call-done), kind=kOutput, calls=%fused_computation.12 | convolution fusion | flops 536576000 | bytes 17367040 | tf_op jit(solution)/shard_map/dot_general | solution.py:24
  281.5 139.7 %all-gather.8.cloned.1.call-done = s32[1280,3200]{1,0:T(8,128)} async-done(((s32[160,3200]{1,0:T(8,128)}), s32[1280,3200]{1,0:T(8,128)}) %all-gather.8.cloned.1.call-update) | async-done | bytes 16384016 | tf_op jit(solution)/shard_map/all_gather | solution.py:156
  421.2 8.1 %fusion.4 = f32[64,3200]{1,0:T(8,128)S(1)} fusion(bf16[64,1280]{1,0:T(8,128)(2,1)S(1)} %slice.88, s32[1280,3200]{1,0:T(8,128)} %all-gather.8.cloned.1.call-done), kind=kOutput, calls=%fused_computation.16 | convolution fusion | flops 536576000 | bytes 17367040 | tf_op jit(solution)/shard_map/dot_general | solution.py:24
  429.3 9.9 %fusion.45 = f32[64,3200]{1,0:T(8,128)S(1)} fusion(f32[64,3200]{1,0:T(8,128)S(1)} %fusion, bf16[64,1280]{1,0:T(8,128)(2,1)S(1)} %slice.89, s32[1280,3200]{1,0:T(8,128)} %all-gather.6.cloned.1.call-done), kind=kOutput, calls=%fused_computation.68 | convolution fusion | flops 536780800 | bytes 18186240 | tf_op jit(solution)/shard_map/dot_general | solution.py:24
  439.3 2.4 fusion.42
  441.7 8.1 %fusion.44 = f32[64,3200]{1,0:T(8,128)S(1)} fusion(f32[64,3200]{1,0:T(8,128)S(1)} %fusion.45, bf16[64,1280]{1,0:T(8,128)(2,1)S(1)} %slice.90, s32[1280,3200]{1,0:T(8,128)} %all-gather.6.cloned.1.call-done), kind=kOutput, calls=%fused_computation.67 | convolution fusion | flops 536780800 | bytes 18186240 | tf_op jit(solution)/shard_map/dot_general | solution.py:24
  449.8 2.6 fusion.41
  452.4 7.6 %fusion.46 = f32[64,3200]{1,0:T(8,128)S(1)} fusion(f32[64,3200]{1,0:T(8,128)S(1)} %fusion.44, bf16[64,1280]{1,0:T(8,128)(2,1)S(1)} %slice.91, s32[1280,3200]{1,0:T(8,128)} %all-gather.6.cloned.1.call-done, f32[3200]{0:T(1024)S(1)} %copy-done.7), kind=kOutput, calls=%fused_computation.69 | convolution fusion | flops 536985600 | bytes 18199040 | tf_op jit(solution)/shard_map/dot_general | solution.py:24
  460.0 2.0 fusion.49
  462.0 3.7 slice.92
  465.7 3.7 slice.93
  469.4 3.7 slice.94
  473.1 4.0 slice.95
  477.1 91.6 %all-gather.10.cloned.1.call-done = s32[800,5120]{1,0:T(8,128)} async-done(((s32[800,640]{1,0:T(8,128)}), s32[800,5120]{1,0:T(8,128)}) %all-gather.10.cloned.1.call-update) | async-done | bytes 16384016 | tf_op jit(solution)/shard_map/all_gather | solution.py:159
  568.7 8.2 %fusion.8 = f32[64,5120]{1,0:T(8,128)S(1)} fusion(bf16[64,800]{1,0:T(8,128)(2,1)S(1)} %slice.92, s32[800,5120]{1,0:T(8,128)} %all-gather.10.cloned.1.call-done), kind=kOutput, calls=%fused_computation.20 | convolution fusion | flops 536576000 | bytes 17797120 | tf_op jit(solution)/shard_map/dot_general | solution.py:24
  576.9 2.1 copy-done
  579.0 2.5 fusion.36
  581.5 2.5 fusion.35
  584.0 2.9 fusion.38
  586.9 24.0 %reduce-scatter.2.cloned.1.call-done = bf16[64,1280]{1,0:T(8,128)(2,1)} async-done(((bf16[64,5120]{1,0:T(8,128)(2,1)}), bf16[64,1280]{1,0:T(8,128)(2,1)}) %reduce-scatter.2.cloned.1.call-update) | async-done | bytes 163856 | tf_op jit(solution)/shard_map/reduce_scatter | solution.py:162
  610.9 1.6 add_convert_fusion
  (82 shorter events, 9.4 us)
Async XLA Ops:
  35.3 4.7 copy-start.1
  40.1 2.1 copy-start.8
  41.1 8.0 %copy-start.11 = (s32[1,16]{1,0:T(1,128)S(1)}, s32[1,16]{1,0:T(1,128)}, u32[]{:S(2)}) copy-start(s32[1,16]{1,0:T(1,128)} %param.26) | copy-start | bytes 196
  43.7 12.7 %copy-start.9 = (f32[128]{0:T(128)S(1)}, f32[128]{0:T(128)}, u32[]{:S(2)}) copy-start(f32[128]{0:T(128)} %param.23) | copy-start | bytes 1540
  43.7 12.8 %copy-start.10 = (f32[128]{0:T(128)S(1)}, f32[128]{0:T(128)}, u32[]{:S(2)}) copy-start(f32[128]{0:T(128)} %param.22) | copy-start | bytes 1540
  43.7 12.3 %all-to-all-start = ((bf16[4,16,1280]{2,1,0:T(8,128)(2,1)}), bf16[4,16,1280]{2,1,0:T(8,128)(2,1)S(1)}, u32[]{:S(2)}, u32[]{:S(2)}) async-start(bf16[4,16,1280]{2,1,0:T(8,128)(2,1)} %bitcast.1), calls=%async_computation | async-start | bytes 327680 | tf_op jit(solution)/shard_map/all_to_all | solution.py:143
  49.1 74.9 %all-gather.12.cloned.1.call-start = ((), (), s32[]{:S(2)}) async-start(), calls=%async_computation.7 | async-start | bytes 3276800 | tf_op jit(solution)/shard_map/all_gather | solution.py:15
  75.1 7.0 %slice-start.4 = ((s8[5242880]{0:T(1024)(128)(4,1)}), s8[4194304]{0:T(1024)(128)(4,1)S(1)}, s32[]{:S(2)}) async-start(s8[5242880]{0:T(1024)(128)(4,1)} %bitcast.50), calls=%async_computation.12 | async-start | bytes 8388608
  78.6 3.5 slice-start.5
  78.6 4.4 copy-start.4
  84.6 41.6 %copy-start.2 = (bf16[64,5120]{1,0:T(8,128)(2,1)S(1)}, bf16[64,5120]{1,0:T(8,128)(2,1)}, u32[]{:S(2)}) copy-start(bf16[64,5120]{1,0:T(8,128)(2,1)} %param.18) | copy-start | bytes 1966084
  84.6 42.0 %copy-start.5 = (f32[5120]{0:T(1024)S(1)}, f32[5120]{0:T(1024)}, u32[]{:S(2)}) copy-start(f32[5120]{0:T(1024)} %param.29) | copy-start | bytes 61444
  84.6 188.9 %all-gather.6.cloned.1.call-start = ((), (), s32[]{:S(2)}) async-start(), calls=%async_computation.3 | async-start | bytes 18432000 | tf_op jit(solution)/shard_map/all_gather | solution.py:154
  85.4 335.8 %all-gather.8.cloned.1.call-start = ((), (), s32[]{:S(2)}) async-start(), calls=%async_computation.4 | async-start | bytes 18432000 | tf_op jit(solution)/shard_map/all_gather | solution.py:156
  86.1 482.6 %all-gather.10.cloned.1.call-start = ((), (), s32[]{:S(2)}) async-start(), calls=%async_computation.5 | async-start | bytes 18432000 | tf_op jit(solution)/shard_map/all_gather | solution.py:159
  86.7 524.3 %reduce-scatter.2.cloned.1.call-start = ((), (), s32[]{:S(2)}) async-start(), calls=%async_computation.6 | async-start | bytes 819200 | tf_op jit(solution)/shard_map/reduce_scatter | solution.py:162
  421.2 18.1 %slice-start = ((s8[16384000]{0:T(1024)(128)(4,1)}), s8[4194304]{0:T(1024)(128)(4,1)S(1)}, s32[]{:S(2)}) async-start(s8[16384000]{0:T(1024)(128)(4,1)} %bitcast.48), calls=%async_computation.8 | async-start | bytes 8388608
  421.2 18.1 %slice-start.1 = ((s8[16384000]{0:T(1024)(128)(4,1)}), s8[4194304]{0:T(1024)(128)(4,1)S(1)}, s32[]{:S(2)}) async-start(s8[16384000]{0:T(1024)(128)(4,1)} %bitcast.48), calls=%async_computation.9 | async-start | bytes 8388608
  429.3 10.0 %slice-start.2 = ((s8[16384000]{0:T(1024)(128)(4,1)}), s8[4194304]{0:T(1024)(128)(4,1)S(1)}, s32[]{:S(2)}) async-start(s8[16384000]{0:T(1024)(128)(4,1)} %bitcast.48), calls=%async_computation.10 | async-start | bytes 8388608
  429.3 10.0 %slice-start.3 = ((s8[16384000]{0:T(1024)(128)(4,1)}), s8[3801088]{0:T(1024)(128)(4,1)S(1)}, s32[]{:S(2)}) async-start(s8[16384000]{0:T(1024)(128)(4,1)} %bitcast.48), calls=%async_computation.11 | async-start | bytes 7602176
  449.7 2.6 copy-start.7
  452.4 7.6 %copy-start.6 = (f32[3200]{0:T(1024)S(1)}, f32[3200]{0:T(1024)}, u32[]{:S(2)}) copy-start(f32[3200]{0:T(1024)} %param.33) | copy-start | bytes 38404
  568.7 10.3 %copy-start = (s32[800,5120]{1,0:T(8,128)S(1)}, s32[800,5120]{1,0:T(8,128)}, u32[]{:S(2)}) copy-start(s32[800,5120]{1,0:T(8,128)} %all-gather.10.cloned.1.call-done) | copy-start | bytes 49152004
  581.5 2.5 copy-start.3
Sparse Core Ops, SparseCore 0:
  84.7 39.2 all-gather.11
  125.6 147.8 all-gather.5
  275.1 146.0 all-gather.7
  422.6 146.0 all-gather.9
  587.1 23.8 reduce-scatter.1
